TPU v7x, 256 devices: a whole 4x4x8 slice. The times are simulated.
256 devices in a mesh: tok: 32 (over z_lo, x, core), blk: 8 (over y, z_hi).
Axes of the slice: x: 4, y: 4, z: 8 (z_hi: 2, z_lo: 4; z = z_hi * 4 + z_lo), core: 2. Of those that a mesh axis runs over, the one named last changes fastest.
Arguments:
- activations: bfloat16 [4096, 7168], P('tok', 'blk'), may hold values from -600 to 600
- signs: float32 [7168], P('blk'), may hold values from -1 to 1, as said below
Outputs:
- hessian: float32 [7168, 7168], P('tok', 'blk')
- incoherence: float32 [7168], P('blk')
- largest_ratio: float32 [], replicated
Inputs may be any that keep to these rules, and one draw needn't show every extreme that they name: `signs`: every entry is -1 or 1.
All inputs are finite; a program needn't handle non-finite values.
Results may differ from a plain program's by a relative error of at most 0.0037.
Values may be sent and summed in bfloat16 or wider, within the bound.
A program may use at most 128 MiB of HBM per device.

v0:
```python
import math
import jax
import jax.numpy as jnp
import numpy as np
from jax import lax
from jax.sharding import PartitionSpec as P

WALSH = 512
MIX = 14
FEATURES = 7168
EPS = 1e-06
DAMP = 0.01


def walsh(length):
    table = np.ones((1, 1))
    while table.shape[0] < length:
        table = np.block([[table, table], [table, -table]])
    return table


def cosine(length):
    k = np.arange(length)[:, None]
    n = np.arange(length)[None, :]
    table = math.sqrt(2.0 / length) * np.cos(math.pi * (n + 0.5) * k / length)
    table[0] *= math.sqrt(0.5)
    return table


def split_table(local):
    table = np.kron(walsh(local), cosine(MIX).T) / math.sqrt(WALSH)
    high = table.astype(jnp.bfloat16)
    low = (table - high.astype(np.float64)).astype(jnp.bfloat16)
    return (high, low)


def contract_tokens(left, right):
    return lax.dot_general(
        left, right, (((0,), (0,)), ((), ())), preferred_element_type=jnp.float32
    )


def combine(parts):
    parts = list(parts)
    step = 1
    while step < len(parts):
        for i in range(0, len(parts), 2 * step):
            for j in range(i, i + step):
                parts[j], parts[j + step] = (parts[j] + parts[j + step], parts[j] - parts[j + step])
        step *= 2
    return parts


def per_device(activations, signs):
    rows, width = activations.shape
    blocks = lax.axis_size("blk")
    toks = lax.axis_size("tok")
    b = lax.axis_index("blk")
    t = lax.axis_index("tok")
    share = rows // blocks
    row_count = FEATURES // toks
    high, low = split_table(WALSH // blocks)
    signed = activations * signs.astype(jnp.bfloat16)[None, :]
    mine = lax.all_to_all(signed.reshape(blocks, share, width), "blk", 0, 0, tiled=True)
    flat = mine.reshape(blocks * share, width)
    mixed = jnp.dot(flat, high, preferred_element_type=jnp.float32)
    mixed = mixed + jnp.dot(flat, low, preferred_element_type=jnp.float32)
    mixed = mixed.reshape(blocks, share, width)
    rotated = jnp.stack(combine([mixed[i] for i in range(blocks)])).astype(jnp.bfloat16)
    wide = rotated.astype(jnp.float32)
    trace_total = lax.psum(jnp.sum(wide * wide), ("tok", "blk"))
    columns = lax.all_to_all(rotated, "blk", 0, 0, tiled=True).reshape(rows, width)
    columns = lax.all_gather(columns, "tok", axis=0, tiled=True)
    pieces = jnp.moveaxis(rotated, 0, 1).reshape(share, toks, row_count)
    pieces = lax.all_to_all(jnp.moveaxis(pieces, 1, 0), "tok", 0, 0, tiled=True)
    pieces = lax.all_gather(pieces, "blk", axis=1, tiled=False)
    left = pieces.reshape(toks * rows, row_count)
    gram = contract_tokens(left, columns)
    at_rows = t * row_count + jnp.arange(row_count, dtype=jnp.int32)[:, None]
    at_columns = b * width + jnp.arange(width, dtype=jnp.int32)[None, :]
    on_diag = at_rows == at_columns
    peaks = jnp.max(jnp.where(on_diag, 0.0, jnp.abs(gram)), axis=0)
    peak = lax.pmax(peaks, "tok")
    largest = lax.pmax(jnp.max(peak), "blk")
    diag_mean = trace_total / FEATURES + EPS
    hessian = gram / diag_mean + DAMP * on_diag.astype(jnp.float32)
    return (hessian, peak / diag_mean, largest / diag_mean)


def solution(mesh):
    return jax.shard_map(
        per_device,
        mesh=mesh,
        in_specs=(P("tok", "blk"), P("blk")),
        out_specs=(P("tok", "blk"), P("blk"), P()),
        check_vma=False,
    )
```

profile of v0, /device:TPU:0, one launch (start us, length us, event | category | flops | bytes accessed | tf_op | source)
XLA Modules:
  0.0 306.4 jit_solution(10132613297484152521)
XLA Ops:
  7.2 0.0 copy-start
  7.2 0.0 all-gather.6.cloned.1.call-start
  7.2 0.8 convert_element_type.8
  8.0 1.0 broadcast_multiply_fusion
  9.0 20.2 %all_to_all.15 = bf16[8,16,896]{2,1,0:T(8,128)(2,1)S(1)} all-to-all(bf16[8,16,896]{2,1,0:T(8,128)(2,1)S(1)} %bitcast.56), channel_id=1, replica_groups=mesh['tok'=32,'blk'=8] {'blk'}, dimensions={0} | all-to-all | bytes 458752 | tf_op jit(solution)/shard_map/all_to_all | solution.py:64
  29.2 1.9 fusion.22
  31.1 0.0 copy-done
  31.1 0.4 convolution_add_fusion
  31.8 0.2 reshape.51
  32.0 0.2 copy.10
  32.2 18.7 %all_to_all.16 = bf16[32,16,224]{2,1,0:T(8,128)(2,1)S(1)} all-to-all(bf16[32,16,224]{2,1,0:T(8,128)(2,1)S(1)} %copy.10), channel_id=1, replica_groups=mesh['tok'=32,'blk'=8] {'tok'}, dimensions={0} | all-to-all | bytes 458752 | tf_op jit(solution)/shard_map/all_to_all | solution.py:75
  50.9 0.8 copy.11
  51.7 0.0 all-gather.6.cloned.1.call-update
  51.8 0.0 all-gather.4.cloned.1.call-start
  51.8 14.7 %all_to_all.17 = bf16[8,16,896]{2,1,0:T(8,128)(2,1)} all-to-all(bf16[8,16,896]{2,1,0:T(8,128)(2,1)S(1)} %fusion.20), channel_id=1, replica_groups=mesh['tok'=32,'blk'=8] {'blk'}, dimensions={0} | all-to-all | bytes 458752 | tf_op jit(solution)/shard_map/all_to_all | solution.py:72
  66.5 0.0 all-gather.4.cloned.1.call-update
  66.6 0.7 multiply_reduce_fusion
  67.3 90.8 %psum.7 = f32[]{:T(128)} all-reduce(f32[]{:T(128)} %multiply_reduce_fusion), channel_id=1, replica_groups=mesh['tok'=32,'blk'=8] {'tok','blk'}, use_global_device_ids=true, to_apply=%region_1.0 | all-reduce | flops 1 | bytes 8 | tf_op jit(solution)/shard_map/psum | solution.py:71
  158.7 0.0 all-gather.6.cloned.1.call-done
  158.7 4.1 %copy.12 = bf16[32,128,224]{1,0,2:T(8,128)(2,1)S(1)} copy(bf16[32,128,224]{2,0,1:T(8,128)(2,1)} %all-gather.6.cloned.1.call-done) | data formatting | bytes 3670016 | tf_op jit(solution)/shard_map/all_gather | solution.py:76
  162.8 26.1 %all-gather.4.cloned.1.call-done = bf16[4096,896]{1,0:T(8,128)(2,1)} async-done(((bf16[128,896]{1,0:T(8,128)(2,1)}), bf16[4096,896]{1,0:T(8,128)(2,1)}) %all-gather.4.cloned.1.call-update) | async-done | bytes 7340048 | tf_op jit(solution)/shard_map/all_gather | solution.py:73
  188.9 6.5 %fusion.4 = (f32[896]{0:T(1024)S(1)}, f32[224,896]{1,0:T(8,128)}) fusion(s32[896]{0:T(1024)S(1)} %iota_add_fusion, s32[224]{0:T(256)S(1)} %iota_add_fusion.1, f32[]{:T(128)S(6)} %add.82, bf16[4096,896]{1,0:T(8,128)(2,1)} %all-gather.4.cloned.1.call-done, bf16[28,8,32,128]{3,2,1,0:T(8,128)(2,1)S(1)} %bitcast.53), kind=kOutput, calls=%fused_computation.7 | convolution fusion | flops 1645571200 | bytes 9985924 | tf_op jit(solution)/shard_map/dot_general | solution.py:38
  195.4 69.8 %pmax.14 = f32[896]{0:T(1024)S(1)} all-reduce(f32[896]{0:T(1024)S(1)} %get-tuple-element.13), channel_id=1, replica_groups=mesh['tok'=32,'blk'=8] {'tok'}, use_global_device_ids=true, to_apply=%region_3.4 | all-reduce | flops 896 | bytes 7168 | tf_op jit(solution)/shard_map/pmax | solution.py:83
  265.3 1.2 fusion.21
  266.5 31.3 %pmax.15 = f32[]{:T(128)} all-reduce(f32[]{:T(128)} %get-tuple-element.15), channel_id=1, replica_groups=mesh['tok'=32,'blk'=8] {'blk'}, use_global_device_ids=true, to_apply=%region_5.6 | all-reduce | flops 1 | bytes 8 | tf_op jit(solution)/shard_map/pmax | solution.py:84
  (11 shorter events, 0.3 us)
Async XLA Ops:
  7.2 23.9 %copy-start = (bf16[896,896]{1,0:T(8,128)(2,1)S(1)}, bf16[896,896]{1,0:T(8,128)(2,1)}, u32[]{:S(2)}) copy-start(bf16[896,896]{1,0:T(8,128)(2,1)} %constant.30.clone) | copy-start | bytes 4816900
  7.2 151.6 %all-gather.6.cloned.1.call-start = ((), (), s32[]{:S(2)}) async-start(), calls=%async_computation.4 | async-start | bytes 2359296 | tf_op jit(solution)/shard_map/all_gather | solution.py:76
  51.8 137.2 %all-gather.4.cloned.1.call-start = ((), (), s32[]{:S(2)}) async-start(), calls=%async_computation.3 | async-start | bytes 7569408 | tf_op jit(solution)/shard_map/all_gather | solution.py:73
Sparse Core Ops, SparseCore 0:
  51.9 71.4 all-gather.5
  125.2 63.6 all-gather.3
where the time goes:
time: 307 us; the launch traced here: 306 us
  blocking collectives  246 us (80%)
  waiting for transfers between devices  26.1 us (9%)
  between operations  16.6 us (5%)
  matrix products  8.8 us (3%)
  local copies, waits for them, and re-layouts  5.31 us (2%)
  other arithmetic  3.89 us (1%)
    psum x1, blocking collectives, per_device(): trace_total = lax.psum(jnp.sum(wide * wide), ('tok', 'blk'))  90.8 us
    pmax x1, blocking collectives, per_device(): peak = lax.pmax(peaks, 'tok')  69.8 us
    pmax x1, blocking collectives, per_device(): largest = lax.pmax(jnp.max(peak), 'blk')  31.3 us
    all_gather x1, waiting for transfers between devices, per_device(): columns = lax.all_gather(columns, 'tok', axis=0, tiled=True)  26.1 us
    all_to_all x1, blocking collectives, per_device(): lax.all_to_all(signed.reshape(blocks, share, width), 'blk', 0, 0, tiled=T...  20.2 us
    all_to_all x1, blocking collectives, per_device(): pieces = lax.all_to_all(jnp.moveaxis(pieces, 1, 0), 'tok', 0, 0, tiled=True)  18.7 us
    all_to_all x1, blocking collectives, per_device(): lax.all_to_all(rotated, 'blk', 0, 0, tiled=True).reshape(rows, width)  14.7 us
    dot_general x1, matrix products, contract_tokens(): lax.dot_general(left, right, (((0,), (0,)), ((), ())), preferred_element_...  6.5 us
  transfers between devices with their start and end apart: 2, of which 1 were waited for; matrix products, arithmetic and copies ran while one was open for 2% of the time, Pallas kernels for 0%

commit v1 on v0

--- a/solution.py
+++ b/solution.py
@@ -70,7 +70,12 @@
     wide = rotated.astype(jnp.float32)
     trace_total = lax.psum(jnp.sum(wide * wide), ("tok", "blk"))
     columns = lax.all_to_all(rotated, "blk", 0, 0, tiled=True).reshape(rows, width)
-    columns = lax.all_gather(columns, "tok", axis=0, tiled=True)
+    columns = jnp.concatenate(
+        lax.all_to_all(
+            jnp.stack([columns for _ in range(lax.axis_size("tok"))], axis=0), "tok", 0, 0
+        ),
+        axis=0,
+    )
     pieces = jnp.moveaxis(rotated, 0, 1).reshape(share, toks, row_count)
     pieces = lax.all_to_all(jnp.moveaxis(pieces, 1, 0), "tok", 0, 0, tiled=True)
     pieces = lax.all_gather(pieces, "blk", axis=1, tiled=False)

time: 307 us -> 431 us (1.40)
  blocking collectives: 246 us -> 367 us
  waiting for transfers between devices: 26.1 us -> 9.66 us
  starting transfers between devices: 0.08 us -> 8.35 us
  other arithmetic: 3.89 us -> 9.64 us
  local copies, waits for them, and re-layouts: 5.31 us -> 10.3 us
    psum x1, blocking collectives: 90.8 us -> 229 us  [per_device(): trace_total = lax.psum(jnp.sum(wide * wide), ('tok', 'blk'))]
    all_gather x1 -> x0, waiting for transfers between devices: 26.1 us -> none  [per_device(): columns = lax.all_gather(columns, 'tok', axis=0, tiled=True)]
    all_to_all x1 -> x0, blocking collectives: 14.7 us -> none  [per_device(): lax.all_to_all(rotated, 'blk', 0, 0, tiled=True).reshape(rows, width)]
    all_to_all x0 -> x2, waiting for transfers between devices: none -> 9.63 us  [the longest x1 9.62 us: per_device(): lax.all_to_all(rotated, 'blk', 0, 0, tiled=True).reshape(rows, width)]
    all_to_all x0 -> x2, starting transfers between devices: none -> 8.31 us  [the longest x1 4.91 us: per_device(): lax.all_to_all(jnp.stack([columns for _ in range(lax.axis_size('tok'))],...]
  transfers between devices with their start and end apart: 2 -> 3, of which waited for: 1 -> 1; matrix products, arithmetic and copies ran while one was open for 2% -> 2% of each run, Pallas kernels for 0% -> 0%
where the time goes in v1:
time: 431 us; the launch traced here: 430 us
  blocking collectives  367 us (85%)
  between operations  16.6 us (4%)
  local copies, waits for them, and re-layouts  10.3 us (2%)
  waiting for transfers between devices  9.66 us (2%)
  other arithmetic  9.64 us (2%)
  matrix products  8.58 us (2%)
  starting transfers between devices  8.35 us (2%)
    psum x1, blocking collectives, per_device(): trace_total = lax.psum(jnp.sum(wide * wide), ('tok', 'blk'))  229 us
    pmax x1, blocking collectives, per_device(): peak = lax.pmax(peaks, 'tok')  70.2 us
    pmax x1, blocking collectives, per_device(): largest = lax.pmax(jnp.max(peak), 'blk')  28 us
    all_to_all x1, blocking collectives, per_device(): lax.all_to_all(signed.reshape(blocks, share, width), 'blk', 0, 0, tiled=T...  20.2 us
    all_to_all x1, blocking collectives, per_device(): pieces = lax.all_to_all(jnp.moveaxis(pieces, 1, 0), 'tok', 0, 0, tiled=True)  19 us
    all_to_all x1, waiting for transfers between devices, per_device(): lax.all_to_all(rotated, 'blk', 0, 0, tiled=True).reshape(rows, width)  9.62 us
  transfers between devices with their start and end apart: 3, of which 1 were waited for; matrix products, arithmetic and copies ran while one was open for 2% of the time, Pallas kernels for 0%

profile of v1, /device:TPU:0, one launch (start us, length us, event | category | flops | bytes accessed | tf_op | source)
XLA Modules:
  0.0 430.0 jit_solution(6528080680008196636)
XLA Ops:
  7.2 0.0 copy-start
  7.2 0.8 convert_element_type.8
  8.0 1.0 broadcast_multiply_fusion
  9.0 20.2 %all_to_all.20 = bf16[8,16,896]{2,1,0:T(8,128)(2,1)S(1)} all-to-all(bf16[8,16,896]{2,1,0:T(8,128)(2,1)S(1)} %bitcast.55), channel_id=1, replica_groups=mesh['tok'=32,'blk'=8] {'blk'}, dimensions={0} | all-to-all | bytes 458752 | tf_op jit(solution)/shard_map/all_to_all | solution.py:64
  29.2 1.9 fusion.22
  31.0 0.0 copy-done
  31.0 0.4 convolution_add_fusion
  31.5 0.6 fusion.6
  32.1 0.6 fusion.8
  32.7 0.6 fusion.10
  33.4 0.6 fusion.12
  34.0 0.6 fusion.14
  34.6 0.6 fusion.16
  35.2 0.6 fusion.18
  35.9 0.6 fusion.20
  36.5 3.4 all-to-all-start.2
  39.9 1.0 copy.9
  40.9 0.2 reshape.53
  41.2 0.2 copy.10
  41.3 9.6 %all-to-all-done.2 = bf16[8,16,896]{2,1,0:T(8,128)(2,1)S(1)} async-done(((bf16[8,16,896]{2,1,0:T(8,128)(2,1)}), bf16[8,16,896]{2,1,0:T(8,128)(2,1)S(1)}, u32[]{:S(2)}, u32[]{:S(2)}) %all-to-all-start.2) | async-done | bytes 229408 | tf_op jit(solution)/shard_map/all_to_all | solution.py:72
  50.9 19.0 %all_to_all.21 = bf16[32,16,224]{2,1,0:T(8,128)(2,1)S(1)} all-to-all(bf16[32,16,224]{2,1,0:T(8,128)(2,1)S(1)} %copy.10), channel_id=1, replica_groups=mesh['tok'=32,'blk'=8] {'tok'}, dimensions={0} | all-to-all | bytes 458752 | tf_op jit(solution)/shard_map/all_to_all | solution.py:80
  69.9 4.1 stack.48
  74.0 4.9 %all-to-all-start.3 = ((bf16[32,128,896]{2,1,0:T(8,128)(2,1)}), bf16[32,128,896]{2,1,0:T(8,128)(2,1)}, u32[]{:S(2)}, u32[]{:S(2)}) async-start(bf16[32,128,896]{2,1,0:T(8,128)(2,1)} %stack.48), calls=%async_computation.3 | async-start | bytes 14680064 | tf_op jit(solution)/shard_map/all_to_all | solution.py:74
  78.9 0.0 all-gather.3.cloned.1.call-start
  78.9 0.8 copy.11
  79.7 0.0 all-gather.3.cloned.1.call-update
  79.8 1.7 multiply_reduce_fusion
  81.4 229.4 %psum.7 = f32[]{:T(128)} all-reduce(f32[]{:T(128)} %multiply_reduce_fusion), channel_id=1, replica_groups=mesh['tok'=32,'blk'=8] {'tok','blk'}, use_global_device_ids=true, to_apply=%region_1.0 | all-reduce | flops 1 | bytes 8 | tf_op jit(solution)/shard_map/psum | solution.py:71
  311.5 0.0 all-gather.3.cloned.1.call-done
  311.5 4.1 copy.12
  315.6 0.0 all-to-all-done.3
  315.6 6.3 %fusion.4 = (f32[896]{0:T(1024)S(1)}, f32[224,896]{1,0:T(8,128)}) fusion(s32[896]{0:T(1024)S(1)} %iota_add_fusion, s32[224]{0:T(256)S(1)} %iota_add_fusion.1, f32[]{:T(128)S(6)} %add.82, bf16[4096,896]{1,0:T(8,128)(2,1)} %bitcast.13, bf16[28,8,32,128]{3,2,1,0:T(8,128)(2,1)S(1)} %bitcast.53), kind=kOutput, calls=%fused_computation.7 | convolution fusion | flops 1645571200 | bytes 9985924 | tf_op jit(solution)/shard_map/dot_general | solution.py:38
  321.9 70.2 %pmax.14 = f32[896]{0:T(1024)S(1)} all-reduce(f32[896]{0:T(1024)S(1)} %get-tuple-element.13), channel_id=1, replica_groups=mesh['tok'=32,'blk'=8] {'tok'}, use_global_device_ids=true, to_apply=%region_3.4 | all-reduce | flops 896 | bytes 7168 | tf_op jit(solution)/shard_map/pmax | solution.py:88
  392.1 1.2 fusion.21
  393.3 28.0 %pmax.15 = f32[]{:T(128)} all-reduce(f32[]{:T(128)} %get-tuple-element.15), channel_id=1, replica_groups=mesh['tok'=32,'blk'=8] {'blk'}, use_global_device_ids=true, to_apply=%region_5.6 | all-reduce | flops 1 | bytes 8 | tf_op jit(solution)/shard_map/pmax | solution.py:89
  (2 shorter events, 0.0 us)
Async XLA Ops:
  7.2 23.9 %copy-start = (bf16[896,896]{1,0:T(8,128)(2,1)S(1)}, bf16[896,896]{1,0:T(8,128)(2,1)}, u32[]{:S(2)}) copy-start(bf16[896,896]{1,0:T(8,128)(2,1)} %constant.30.clone) | copy-start | bytes 4816900
  36.5 14.5 %all-to-all-start.2 = ((bf16[8,16,896]{2,1,0:T(8,128)(2,1)}), bf16[8,16,896]{2,1,0:T(8,128)(2,1)S(1)}, u32[]{:S(2)}, u32[]{:S(2)}) async-start(bf16[8,16,896]{2,1,0:T(8,128)(2,1)} %fusion.20), calls=%async_computation.2 | async-start | bytes 458752 | tf_op jit(solution)/shard_map/all_to_all | solution.py:72
  74.0 241.6 %all-to-all-start.3 = ((bf16[32,128,896]{2,1,0:T(8,128)(2,1)}), bf16[32,128,896]{2,1,0:T(8,128)(2,1)}, u32[]{:S(2)}, u32[]{:S(2)}) async-start(bf16[32,128,896]{2,1,0:T(8,128)(2,1)} %stack.48), calls=%async_computation.3 | async-start | bytes 14680064 | tf_op jit(solution)/shard_map/all_to_all | solution.py:74
  78.9 232.6 %all-gather.3.cloned.1.call-start = ((), (), s32[]{:S(2)}) async-start(), calls=%async_computation.4 | async-start | bytes 2359296 | tf_op jit(solution)/shard_map/all_gather | solution.py:81
Sparse Core Ops, SparseCore 0:
  82.9 88.9 all-gather.2
